TPU v7x, 32 devices: a whole 2x2x4 slice. The times are simulated.
32 devices in a mesh: ao: 8 (over y, x, core), aux: 4 (over z).
Axes of the slice: x: 2, y: 2, z: 4, core: 2. Of those that a mesh axis runs over, the one named last changes fastest.
Arguments:
- blocks: bfloat16 [48, 256, 128, 128], P('ao', 'aux'), may hold values from -6 to 6
- pairs: int32 [48, 2], P('ao'), may hold values from 0 to 79, as said below
- counts: int32 [8], P('ao'), may hold values from 1 to 6, as said below
- owned_blocks: int32 [80], P('ao'), may hold values from 0 to 79, as said below
- occ_coef: bfloat16 [80, 8, 128], P('ao'), may hold values from -0.5 to 0.5
- vir_coef: bfloat16 [10240, 9216], P('ao', 'aux'), may hold values from -0.109375 to 0.109375
Outputs:
- b_tensor: bfloat16 [256, 8, 9216], P('ao', None, 'aux')
Inputs may be any that keep to these rules, and one draw needn't show every extreme that they name: `pairs`: among the used slots of one ao index, at most 3 have nu blocks whose rows one owner holds; in every draw some index reaches 3. `counts`: some ao index uses all 6 slots in every draw. `owned_blocks`: every atom block appears exactly once.
All inputs are finite; a program needn't handle non-finite values.
Results may differ from a plain program's by a relative error of at most 0.014.
Values may be sent and summed in bfloat16 or wider, within the bound.
A program may use at most 128 MiB of HBM per device.

v0:
```python
import jax
import jax.numpy as jnp
from jax import lax
from jax.sharding import PartitionSpec as P


def block_place(block_ids, owned_all):
    hits = block_ids[..., None] == owned_all
    positions = jnp.arange(owned_all.shape[0], dtype=jnp.int32)
    return jnp.sum(jnp.where(hits, positions, 0), axis=-1)


def per_device(blocks, pairs, counts, owned_blocks, occ_coef, vir_coef):
    groups = lax.axis_size("ao")
    own_index = lax.axis_index("ao")
    slot_count = blocks.shape[0]
    aux_depth = blocks.shape[1]
    block_width = blocks.shape[3]
    occupied = occ_coef.shape[1]
    all_pairs, all_counts, all_owned = (
        lax.all_gather(pairs, "ao", axis=0, tiled=True),
        lax.all_gather(counts, "ao", axis=0, tiled=True),
        lax.all_gather(owned_blocks, "ao", axis=0, tiled=True),
    )
    occ_all = lax.all_gather(occ_coef, "ao", axis=0, tiled=True)
    total_blocks = all_owned.shape[0]
    per_owner = total_blocks // groups
    slot_ids = jnp.arange(slot_count, dtype=jnp.int32)
    in_use = slot_ids < counts[0]
    occ_pick = occ_all[block_place(pairs[:, 0], all_owned)]
    slab_values = jnp.einsum("sim,spmn->spin", occ_pick, blocks, preferred_element_type=jnp.float32)
    slab_values = jnp.where(in_use[:, None, None, None], slab_values, 0.0).astype(jnp.bfloat16)
    flat_slabs = slab_values.reshape(slot_count, aux_depth * occupied, block_width)
    place_all = block_place(all_pairs[:, 1], all_owned).reshape(groups, slot_count)
    owner_all = place_all // per_owner
    local_all = place_all % per_owner
    live_all = slot_ids[None, :] < all_counts[:, None]
    mine_all = live_all & (owner_all == own_index)
    local_ids = jnp.arange(per_owner, dtype=jnp.int32)
    slabs_got = lax.all_gather(flat_slabs, "ao", axis=0, tiled=True)
    assign = (
        mine_all.reshape(-1)[None, :] & (local_all.reshape(-1)[None, :] == local_ids[:, None])
    ).astype(jnp.bfloat16)
    summed = jnp.einsum("lt,tqm->qlm", assign, slabs_got, preferred_element_type=jnp.float32)
    rows_local = summed.reshape(summed.shape[0], per_owner * block_width).astype(jnp.bfloat16)
    rows_whole = lax.all_gather(rows_local, "aux", axis=0, tiled=True)
    share = rows_whole.shape[0] // groups
    result = lax.psum_scatter(
        jnp.dot(rows_whole, vir_coef, preferred_element_type=jnp.float32).astype(jnp.bfloat16),
        "ao",
        scatter_dimension=0,
        tiled=True,
    ).astype(jnp.float32)
    return result.reshape(share // occupied, occupied, vir_coef.shape[1]).astype(jnp.bfloat16)


def solution(mesh):
    in_specs = (
        P("ao", "aux", None, None),
        P("ao", None),
        P("ao"),
        P("ao"),
        P("ao", None, None),
        P("ao", "aux"),
    )
    out_specs = P("ao", None, "aux")
    return jax.shard_map(
        per_device, mesh=mesh, in_specs=in_specs, out_specs=out_specs, check_vma=False
    )
```

profile of v0, /device:TPU:0, one launch (start us, length us, event | category | flops | bytes accessed | tf_op | source)
XLA Modules:
  0.0 291.0 jit_solution(9892513670469097050)
XLA Ops:
  7.2 0.7 slice_bitcast_fusion.1
  7.9 1.3 dynamic-slice
  9.9 0.8 dynamic-update-slice.1
  10.7 0.8 dynamic-update-slice
  11.5 9.5 %all-reduce.2 = (s32[80]{0:T(128)S(1)}, s32[8]{0:T(128)S(1)}) all-reduce(s32[80]{0:T(128)S(1)} %dynamic-update-slice, s32[8]{0:T(128)S(1)} %dynamic-update-slice.1), channel_id=1, replica_groups=mesh['ao'=8,'aux'=4] {'ao'}, use_global_device_ids=true, to_apply=%add | all-reduce | flops 88 | bytes 704
  21.0 0.2 select_reduce_fusion.1
  21.2 8.6 %all_gather.18 = bf16[80,8,128]{2,1,0:T(8,128)(2,1)S(1)} all-gather(bf16[10,8,128]{2,1,0:T(8,128)(2,1)} %param.10), channel_id=1, replica_groups=mesh['ao'=8,'aux'=4] {'ao'}, dimensions={0}, use_global_device_ids=true | all-gather | bytes 184320 | tf_op jit(solution)/shard_map/all_gather | solution.py:25
  29.8 0.6 gather_fusion
  30.4 7.2 %fusion.4 = bf16[6,512,128]{2,1,0:T(8,128)(2,1)} fusion(bf16[6,64,128,128]{3,2,1,0:T(8,128)(2,1)} %param.6, pred[6]{0:T(512)(128)(4,1)S(1)} %iota_compare_fusion.2, bf16[6,8,128]{2,1,0:T(8,128)(2,1)S(1)} %gather_fusion), kind=kOutput, calls=%fused_computation.6 | convolution fusion | flops 101449728 | bytes 13381638 | tf_op jit(solution)/shard_map/sim,spmn->spin/dot_general | solution.py:31
  37.6 0.0 all-gather.4.cloned.1.call-update
  37.6 0.0 all-gather.6.cloned.1.call-start
  37.7 0.1 iota_compare_fusion.1
  37.8 0.1 lt.52
  37.9 8.6 %all-gather = s32[8,6,2]{1,2,0:T(2,128)S(1)} all-gather(s32[1,6,2]{1,2,0:T(2,128)S(1)} %bitcast.35), channel_id=1, replica_groups=mesh['ao'=8,'aux'=4] {'ao'}, dimensions={0}, use_global_device_ids=true | all-gather | bytes 432 | tf_op jit(solution)/shard_map/all_gather | solution.py:21
  46.5 0.1 reshape.75
  46.5 0.2 select_reduce_fusion
  46.8 36.7 %all-gather.4.cloned.1.call-done = bf16[48,512,128]{2,1,0:T(8,128)(2,1)} async-done(((bf16[6,512,128]{2,1,0:T(8,128)(2,1)}), bf16[48,512,128]{2,1,0:T(8,128)(2,1)}) %all-gather.4.cloned.1.call-update) | async-done | bytes 6291472 | tf_op jit(solution)/shard_map/all_gather | solution.py:40
  83.5 6.4 %convert_bitcast_fusion = bf16[512,10,128]{2,1,0:T(8,128)(2,1)S(1)} fusion(bf16[48,512,128]{2,1,0:T(8,128)(2,1)} %all-gather.4.cloned.1.call-done, s32[48]{0:T(128)S(1)} %and_select_fusion, pred[48]{0:T(512)(128)(4,1)S(1)} %compare_and_fusion), kind=kOutput, calls=%fused_computation.4 | convolution fusion | flops 63570880 | bytes 7602416 | tf_op jit(solution)/shard_map/lt,tqm->qlm/dot_general | solution.py:44
  89.9 2.6 copy.17
  92.5 0.0 all-gather.6.cloned.1.call-update
  92.5 0.2 reduce-scatter.2.cloned.1.call-start
  92.7 98.0 %all-gather.6.cloned.1.call-done = bf16[2048,1280]{0,1:T(8,128)(2,1)} async-done(((bf16[512,1280]{0,1:T(8,128)(2,1)}), bf16[2048,1280]{0,1:T(8,128)(2,1)}) %all-gather.6.cloned.1.call-update) | async-done | bytes 5242896 | tf_op jit(solution)/shard_map/all_gather | solution.py:46
  190.7 18.4 %convolution_convert_fusion = bf16[2048,2304]{1,0:T(8,128)(2,1)} fusion(bf16[2048,1280]{0,1:T(8,128)(2,1)} %all-gather.6.cloned.1.call-done, bf16[1280,2304]{1,0:T(8,128)(2,1)} %param.11), kind=kOutput, calls=%fused_computation.1 | convolution fusion | flops 12084314112 | bytes 20578304 | tf_op jit(solution)/shard_map/dot_general | solution.py:49
  209.1 75.3 %reduce-scatter.2.cloned.1.call-done = bf16[256,2304]{1,0:T(8,128)(2,1)} async-done(((bf16[2048,2304]{1,0:T(8,128)(2,1)}), bf16[256,2304]{1,0:T(8,128)(2,1)}) %reduce-scatter.2.cloned.1.call-update) | async-done | bytes 1179664 | tf_op jit(solution)/shard_map/reduce_scatter | solution.py:48
  (13 shorter events, 0.1 us)
Async XLA Ops:
  6.5 76.9 %all-gather.4.cloned.1.call-start = ((), (), s32[]{:S(2)}) async-start(), calls=%async_computation.1 | async-start | bytes 7077888 | tf_op jit(solution)/shard_map/all_gather | solution.py:40
  30.4 7.5 %copy-start = (s32[6,2]{0,1:T(2,128)S(1)}, s32[6,2]{0,1:T(2,128)}, u32[]{:S(2)}) copy-start(s32[6,2]{0,1:T(2,128)} %param.7) | copy-start | bytes 148
  37.6 153.0 %all-gather.6.cloned.1.call-start = ((), (), s32[]{:S(2)}) async-start(), calls=%async_computation.2 | async-start | bytes 6553600 | tf_op jit(solution)/shard_map/all_gather | solution.py:46
  92.5 191.9 %reduce-scatter.2.cloned.1.call-start = ((), (), s32[]{:S(2)}) async-start(), calls=%async_computation.3 | async-start | bytes 10616832 | tf_op jit(solution)/shard_map/reduce_scatter | solution.py:48
Sparse Core Ops, SparseCore 0:
  37.8 45.6 all-gather.3
  92.6 98.0 all-gather.5
  209.2 75.1 reduce-scatter.1
where the time goes:
time: 291 us
  waiting for transfers between devices  210 us (72%)
  matrix products  32.1 us (11%)
  blocking collectives  26.7 us (9%)
  between operations  14.5 us (5%)
  local copies, waits for them, and re-layouts  6.95 us (2%)
    all_gather x1, waiting for transfers between devices, per_device(): rows_whole = lax.all_gather(rows_local, 'aux', axis=0, tiled=True)  98 us
    reduce_scatter x1, waiting for transfers between devices, per_device(): lax.psum_scatter(jnp.dot(rows_whole, vir_coef, preferred_element_type=jnp...  75.3 us
    all_gather x1, waiting for transfers between devices, per_device(): slabs_got = lax.all_gather(flat_slabs, 'ao', axis=0, tiled=True)  36.7 us
    dot_general x1, matrix products, per_device(): jnp.dot(rows_whole, vir_coef, preferred_element_type=jnp.float32)  18.4 us
    unnamed x1, blocking collectives  9.49 us
    all_gather x1, blocking collectives, per_device(): occ_all = lax.all_gather(occ_coef, 'ao', axis=0, tiled=True)  8.6 us
    all_gather x1, blocking collectives, per_device(): lax.all_gather(pairs, 'ao', axis=0, tiled=True)  8.59 us
    dot_general x1, matrix products, per_device(): jnp.einsum('sim,spmn->spin', occ_pick, blocks, preferred_element_type=jnp...  7.2 us
  transfers between devices with their start and end apart: 3, of which 3 were waited for; matrix products, arithmetic and copies ran while one was open for 0% of the time, Pallas kernels for 0%

commit v1 on v0

--- a/solution.py
+++ b/solution.py
@@ -2,6 +2,27 @@
 import jax.numpy as jnp
 from jax import lax
 from jax.sharding import PartitionSpec as P
+
+
+def pair_tables(vals, u_in):
+    net_axis = "ao"
+    side_arr, built, plain = (
+        jax.lax.axis_size(net_axis),
+        jax.lax.axis_index(net_axis),
+        vals.shape[0],
+    )
+    tray = [(dev_i, (dev_i + 1) % side_arr) for dev_i in range(side_arr)]
+    shelf = [(dev_i, (dev_i - 1) % side_arr) for dev_i in range(side_arr)]
+    shaped = side_arr // 2
+    y = z2 = vals
+    formed = u_in(vals, built * plain)
+    for b in range(1, shaped + 1):
+        y = jax.lax.ppermute(y, axis_name=net_axis, perm=tray)
+        if b < side_arr - shaped:
+            z2 = jax.lax.ppermute(z2, axis_name=net_axis, perm=shelf)
+            formed = formed + u_in(z2, (built + b) % side_arr * plain)
+        formed = formed + u_in(y, (built - b) % side_arr * plain)
+    return formed
 
 
 def block_place(block_ids, owned_all):
@@ -37,11 +58,18 @@
     live_all = slot_ids[None, :] < all_counts[:, None]
     mine_all = live_all & (owner_all == own_index)
     local_ids = jnp.arange(per_owner, dtype=jnp.int32)
-    slabs_got = lax.all_gather(flat_slabs, "ao", axis=0, tiled=True)
     assign = (
         mine_all.reshape(-1)[None, :] & (local_all.reshape(-1)[None, :] == local_ids[:, None])
     ).astype(jnp.bfloat16)
-    summed = jnp.einsum("lt,tqm->qlm", assign, slabs_got, preferred_element_type=jnp.float32)
+    summed = pair_tables(
+        flat_slabs,
+        lambda shard, start: jnp.einsum(
+            "lt,tqm->qlm",
+            lax.dynamic_slice_in_dim(assign, start, shard.shape[0], axis=1),
+            shard,
+            preferred_element_type=jnp.float32,
+        ),
+    )
     rows_local = summed.reshape(summed.shape[0], per_owner * block_width).astype(jnp.bfloat16)
     rows_whole = lax.all_gather(rows_local, "aux", axis=0, tiled=True)
     share = rows_whole.shape[0] // groups

time: 291 us -> 322 us (1.11)
  matrix products: 32.1 us -> 48.1 us
  blocking collectives: 26.7 us -> 37.7 us
  starting transfers between devices: 0.27 us -> 8.35 us
  waiting for transfers between devices: 210 us -> 204 us
    all_gather x1 -> x0, waiting for transfers between devices: 36.7 us -> none  [per_device(): slabs_got = lax.all_gather(flat_slabs, 'ao', axis=0, tiled=True)]
    ppermute x0 -> x7, waiting for transfers between devices: none -> 31.2 us  [the longest x4 31.2 us: pair_tables(): y = jax.lax.ppermute(y, axis_name=net_axis, perm=tray)]
    dot_general x1 -> x8, matrix products: 6.43 us -> 23.4 us  [per_device(): jnp.einsum('lt,tqm->qlm', lax.dynamic_slice_in_dim(assign, start, shard.s...]
    all_gather x1, blocking collectives: 8.59 us -> 19.6 us  [per_device(): lax.all_gather(pairs, 'ao', axis=0, tiled=True)]
    ppermute x0 -> x7, starting transfers between devices: none -> 8.12 us  [the longest x3 7.34 us: pair_tables(): z2 = jax.lax.ppermute(z2, axis_name=net_axis, perm=shelf)]
  transfers between devices with their start and end apart: 3 -> 9, of which waited for: 3 -> 5; matrix products, arithmetic and copies ran while one was open for 0% -> 5% of each run, Pallas kernels for 0% -> 0%
where the time goes in v1:
time: 322 us
  waiting for transfers between devices  204 us (63%)
  matrix products  48.1 us (15%)
  blocking collectives  37.7 us (12%)
  between operations  14.8 us (5%)
  local copies, waits for them, and re-layouts  8.45 us (3%)
  starting transfers between devices  8.35 us (3%)
    all_gather x1, waiting for transfers between devices, per_device(): rows_whole = lax.all_gather(rows_local, 'aux', axis=0, tiled=True)  97.3 us
    reduce_scatter x1, waiting for transfers between devices, per_device(): lax.psum_scatter(jnp.dot(rows_whole, vir_coef, preferred_element_type=jnp...  75.3 us
    ppermute x4, waiting for transfers between devices, pair_tables(): y = jax.lax.ppermute(y, axis_name=net_axis, perm=tray)  31.2 us
    dot_general x8, matrix products, per_device(): jnp.einsum('lt,tqm->qlm', lax.dynamic_slice_in_dim(assign, start, shard.s...  23.4 us
    all_gather x1, blocking collectives, per_device(): lax.all_gather(pairs, 'ao', axis=0, tiled=True)  19.6 us
    dot_general x1, matrix products, per_device(): jnp.dot(rows_whole, vir_coef, preferred_element_type=jnp.float32)  18.4 us
    unnamed x1, blocking collectives  9.49 us
    all_gather x1, blocking collectives, per_device(): occ_all = lax.all_gather(occ_coef, 'ao', axis=0, tiled=True)  8.6 us
  transfers between devices with their start and end apart: 9, of which 5 were waited for; matrix products, arithmetic and copies ran while one was open for 5% of the time, Pallas kernels for 0%

profile of v1, /device:TPU:0, one launch (start us, length us, event | category | flops | bytes accessed | tf_op | source)
XLA Modules:
  0.0 321.8 jit_solution(14239300980116273984)
XLA Ops:
  7.9 1.2 dynamic-slice
  10.5 0.8 dynamic-update-slice
  11.3 9.5 %all-reduce.2 = (s32[80]{0:T(128)S(1)}, s32[8]{0:T(128)S(1)}) all-reduce(s32[80]{0:T(128)S(1)} %dynamic-update-slice, s32[8]{0:T(128)S(1)} %dynamic-update-slice.1), channel_id=1, replica_groups=mesh['ao'=8,'aux'=4] {'ao'}, use_global_device_ids=true, to_apply=%add | all-reduce | flops 88 | bytes 704
  21.0 8.6 %all_gather.15 = bf16[80,8,128]{2,1,0:T(8,128)(2,1)S(1)} all-gather(bf16[10,8,128]{2,1,0:T(8,128)(2,1)} %param.10), channel_id=1, replica_groups=mesh['ao'=8,'aux'=4] {'ao'}, dimensions={0}, use_global_device_ids=true | all-gather | bytes 184320 | tf_op jit(solution)/shard_map/all_gather | solution.py:46
  30.2 6.3 %fusion.1 = bf16[6,512,128]{2,1,0:T(8,128)(2,1)S(1)} fusion(bf16[6,64,128,128]{3,2,1,0:T(8,128)(2,1)} %param.6, pred[6]{0:T(512)(128)(4,1)S(1)} %iota_compare_fusion.2, bf16[6,8,128]{2,1,0:T(8,128)(2,1)S(1)} %gather_fusion), kind=kOutput, calls=%fused_computation.5 | convolution fusion | flops 101449728 | bytes 13381638 | tf_op jit(solution)/shard_map/sim,spmn->spin/dot_general | solution.py:52
  36.9 2.3 collective-permute-start
  39.2 19.6 %all-gather = s32[8,6,2]{1,2,0:T(2,128)S(1)} all-gather(s32[1,6,2]{1,2,0:T(2,128)S(1)} %bitcast.56), channel_id=1, replica_groups=mesh['ao'=8,'aux'=4] {'ao'}, dimensions={0}, use_global_device_ids=true | all-gather | bytes 432 | tf_op jit(solution)/shard_map/all_gather | solution.py:42
  59.8 2.4 collective-permute-start.2
  62.1 2.7 fusion.15
  64.8 13.9 %collective-permute-done.3 = bf16[6,512,128]{2,1,0:T(8,128)(2,1)S(1)} collective-permute-done((bf16[6,512,128]{2,1,0:T(8,128)(2,1)S(1)}, bf16[6,512,128]{2,1,0:T(8,128)(2,1)S(1)}, u32[]{:S(2)}, u32[]{:S(2)}) %collective-permute-start.3) | collective-permute-done | bytes 786464 | tf_op jit(solution)/shard_map/ppermute | solution.py:20
  78.7 0.8 fusion.13
  79.5 0.8 fusion.11
  80.3 2.7 collective-permute-start.4
  83.0 1.9 fusion.9
  84.9 13.0 %collective-permute-done.5 = bf16[6,512,128]{2,1,0:T(8,128)(2,1)S(1)} collective-permute-done((bf16[6,512,128]{2,1,0:T(8,128)(2,1)S(1)}, bf16[6,512,128]{2,1,0:T(8,128)(2,1)S(1)}, u32[]{:S(2)}, u32[]{:S(2)}) %collective-permute-start.5) | collective-permute-done | bytes 786464 | tf_op jit(solution)/shard_map/ppermute | solution.py:20
  97.9 2.7 fusion.7
  100.7 2.7 fusion.3
  103.4 2.7 fusion.5
  106.1 4.2 %collective-permute-done.6 = bf16[6,512,128]{2,1,0:T(8,128)(2,1)} collective-permute-done((bf16[6,512,128]{2,1,0:T(8,128)(2,1)S(1)}, bf16[6,512,128]{2,1,0:T(8,128)(2,1)}, u32[]{:S(2)}, u32[]{:S(2)}) %collective-permute-start.6) | collective-permute-done | bytes 786464 | tf_op jit(solution)/shard_map/ppermute | solution.py:20
  110.4 9.1 %fusion = bf16[512,10,128]{2,1,0:T(8,128)(2,1)} fusion(f32[512,128,10]{1,2,0:T(8,128)} %fusion.3, f32[512,128,10]{1,2,0:T(8,128)} %fusion.5, f32[512,128,10]{1,2,0:T(8,128)} %fusion.7, f32[512,128,10]{1,2,0:T(8,128)S(1)} %fusion.9, f32[512,128,10]{1,2,0:T(8,128)S(1)} %fusion.11, f32[512,128,10]{1,2,0:T(8,128)S(1)} %copy-done, ...), kind=kOutput, calls=%fused_computation.3 | convolution fusion | flops 13107200 | bytes 26739716 | tf_op jit(solution)/shard_map/lt,tqm->qlm/dot_general | solution.py:66
  119.4 4.2 %copy.35 = bf16[512,10,128]{0,2,1:T(8,128)(2,1)} copy(bf16[512,10,128]{2,1,0:T(8,128)(2,1)} %fusion) | data formatting | bytes 2621440 | tf_op jit(solution)/shard_map/convert_element_type | solution.py:73
  123.9 97.3 %all-gather.3.cloned.1.call-done = bf16[2048,1280]{0,1:T(8,128)(2,1)} async-done(((bf16[512,1280]{0,1:T(8,128)(2,1)}), bf16[2048,1280]{0,1:T(8,128)(2,1)}) %all-gather.3.cloned.1.call-update) | async-done | bytes 5242896 | tf_op jit(solution)/shard_map/all_gather | solution.py:74
  221.2 18.4 %convolution_convert_fusion = bf16[2048,2304]{1,0:T(8,128)(2,1)} fusion(bf16[2048,1280]{0,1:T(8,128)(2,1)} %all-gather.3.cloned.1.call-done, bf16[1280,2304]{1,0:T(8,128)(2,1)} %param.11), kind=kOutput, calls=%fused_computation.1 | convolution fusion | flops 12084314112 | bytes 20578304 | tf_op jit(solution)/shard_map/dot_general | solution.py:77
  239.7 75.3 %reduce-scatter.2.cloned.1.call-done = bf16[256,2304]{1,0:T(8,128)(2,1)} async-done(((bf16[2048,2304]{1,0:T(8,128)(2,1)}), bf16[256,2304]{1,0:T(8,128)(2,1)}) %reduce-scatter.2.cloned.1.call-update) | async-done | bytes 1179664 | tf_op jit(solution)/shard_map/reduce_scatter | solution.py:76
  (34 shorter events, 3.8 us)
Async XLA Ops:
  6.5 214.7 %all-gather.3.cloned.1.call-start = ((), (), s32[]{:S(2)}) async-start(), calls=%async_computation.1 | async-start | bytes 6553600 | tf_op jit(solution)/shard_map/all_gather | solution.py:74
  30.2 9.0 %copy-start.1 = (s32[6,2]{0,1:T(2,128)S(1)}, s32[6,2]{0,1:T(2,128)}, u32[]{:S(2)}) copy-start(s32[6,2]{0,1:T(2,128)} %param.7) | copy-start | bytes 148
  36.5 22.8 %collective-permute-start.1 = (bf16[6,512,128]{2,1,0:T(8,128)(2,1)S(1)}, bf16[6,512,128]{2,1,0:T(8,128)(2,1)S(1)}, u32[]{:S(2)}, u32[]{:S(2)}) collective-permute-start(bf16[6,512,128]{2,1,0:T(8,128)(2,1)S(1)} %fusion.1), channel_id=1, source_target_pairs={{0,4},{4,8},{8,12},{12,16},{16,20},{20,24},{24,28},{28,0},{1,5},{5... | collective-permute-start | bytes 2359304 | tf_op jit(solution)/shard_map/ppermute | solution.py:20
  36.9 22.9 %collective-permute-start = (bf16[6,512,128]{2,1,0:T(8,128)(2,1)S(1)}, bf16[6,512,128]{2,1,0:T(8,128)(2,1)S(1)}, u32[]{:S(2)}, u32[]{:S(2)}) collective-permute-start(bf16[6,512,128]{2,1,0:T(8,128)(2,1)S(1)} %fusion.1), channel_id=1, source_target_pairs={{0,28},{4,0},{8,4},{12,8},{16,12},{20,16},{24,20},{28,24},{1,29},{... | collective-permute-start | bytes 2359304 | tf_op jit(solution)/shard_map/ppermute | solution.py:22
  59.3 19.5 %collective-permute-start.3 = (bf16[6,512,128]{2,1,0:T(8,128)(2,1)S(1)}, bf16[6,512,128]{2,1,0:T(8,128)(2,1)S(1)}, u32[]{:S(2)}, u32[]{:S(2)}) collective-permute-start(bf16[6,512,128]{2,1,0:T(8,128)(2,1)S(1)} %collective-permute-done.1), channel_id=1, source_target_pairs={{0,4},{4,8},{8,12},{12,16},{16,20},{20,24},{24,28},{28,0},{1,5},{5... | collective-permute-start | bytes 2359304 | tf_op jit(solution)/shard_map/ppermute | solution.py:20
  59.8 20.5 %collective-permute-start.2 = (bf16[6,512,128]{2,1,0:T(8,128)(2,1)S(1)}, bf16[6,512,128]{2,1,0:T(8,128)(2,1)}, u32[]{:S(2)}, u32[]{:S(2)}) collective-permute-start(bf16[6,512,128]{2,1,0:T(8,128)(2,1)S(1)} %collective-permute-done), channel_id=1, source_target_pairs={{0,28},{4,0},{8,4},{12,8},{16,12},{20,16},{24,20},{28,24},{1,29},{... | collective-permute-start | bytes 2359304 | tf_op jit(solution)/shard_map/ppermute | solution.py:22
  78.7 19.2 %collective-permute-start.5 = (bf16[6,512,128]{2,1,0:T(8,128)(2,1)S(1)}, bf16[6,512,128]{2,1,0:T(8,128)(2,1)S(1)}, u32[]{:S(2)}, u32[]{:S(2)}) collective-permute-start(bf16[6,512,128]{2,1,0:T(8,128)(2,1)S(1)} %collective-permute-done.3), channel_id=1, source_target_pairs={{0,4},{4,8},{8,12},{12,16},{16,20},{20,24},{24,28},{28,0},{1,5},{5... | collective-permute-start | bytes 2359304 | tf_op jit(solution)/shard_map/ppermute | solution.py:20
  80.3 23.1 %collective-permute-start.4 = (bf16[6,512,128]{2,1,0:T(8,128)(2,1)}, bf16[6,512,128]{2,1,0:T(8,128)(2,1)S(1)}, u32[]{:S(2)}, u32[]{:S(2)}) collective-permute-start(bf16[6,512,128]{2,1,0:T(8,128)(2,1)} %collective-permute-done.2), channel_id=1, source_target_pairs={{0,28},{4,0},{8,4},{12,8},{16,12},{20,16},{24,20},{28,24},{1,29},{... | collective-permute-start | bytes 2359304 | tf_op jit(solution)/shard_map/ppermute | solution.py:22
  97.9 12.4 %collective-permute-start.6 = (bf16[6,512,128]{2,1,0:T(8,128)(2,1)S(1)}, bf16[6,512,128]{2,1,0:T(8,128)(2,1)}, u32[]{:S(2)}, u32[]{:S(2)}) collective-permute-start(bf16[6,512,128]{2,1,0:T(8,128)(2,1)S(1)} %collective-permute-done.5), channel_id=1, source_target_pairs={{0,4},{4,8},{8,12},{12,16},{16,20},{20,24},{24,28},{28,0},{1,5},{5... | collective-permute-start | bytes 2359304 | tf_op jit(solution)/shard_map/ppermute | solution.py:20
  100.7 9.7 %copy-start = (f32[512,128,10]{1,2,0:T(8,128)S(1)}, f32[512,128,10]{1,2,0:T(8,128)}, u32[]{:S(2)}) copy-start(f32[512,128,10]{1,2,0:T(8,128)} %fusion.15) | copy-start | bytes 7864324
  123.7 191.3 %reduce-scatter.2.cloned.1.call-start = ((), (), s32[]{:S(2)}) async-start(), calls=%async_computation.2 | async-start | bytes 10616832 | tf_op jit(solution)/shard_map/reduce_scatter | solution.py:76
Sparse Core Ops, SparseCore 0:
  123.8 97.3 all-gather.2
  239.8 75.1 reduce-scatter.1
